TPU v7x, 16 devices: a 4x2x1 block of a 4x4x8 slice. The times are simulated.
16 devices in a mesh: dp: 2 (over y, z), ep: 8 (over x, core).
Axes of the slice: x: 4, y: 2, z: 1, core: 2. Of those that a mesh axis runs over, the one named last changes fastest.
The devices are a block of a 4x4x8 slice.
Arguments:
- hidden: bfloat16 [3072, 2560], P(('dp', 'ep')), parts along dimension 0
- route_idx: int32 [3072, 6], P(('dp', 'ep')), parts along dimension 0
- gate_weights: float32 [3072, 6], P(('dp', 'ep')), parts along dimension 0
- w_gate: bfloat16 [64, 2560, 1536], P('ep')
- w_up: bfloat16 [64, 2560, 1536], P('ep')
- w_down: bfloat16 [64, 1536, 2560], P('ep')
Outputs:
- output: bfloat16 [3072, 2560], P(('dp', 'ep')), parts along dimension 0
There are 2 independent parts. A program takes and returns all parts, laid end to end along the dimension named above; an argument that names none is the same for every part.
All inputs are finite; a program needn't handle non-finite values.
Results may differ from a plain program's by a relative error of at most 0.00119.
Values are sent between devices in bfloat16 or wider.
A program may use at most 768 MiB of HBM per device.

v0:
```python
import jax
import jax.numpy as jnp
from jax import lax
from jax.sharding import PartitionSpec as P, NamedSharding


def pair_plan(route_rows, num_experts, row_cap):
    tok_count, top_k = route_rows.shape
    flat_ids = route_rows.reshape(-1)
    sort_order = jnp.argsort(flat_ids, stable=True)
    counts = jnp.bincount(flat_ids, length=num_experts)
    starts = jnp.cumsum(counts) - counts
    slot_range = jnp.arange(row_cap)
    pair_pos = jnp.minimum(starts[:, None] + slot_range[None, :], tok_count * top_k - 1)
    src_rows = sort_order[pair_pos] // top_k
    pair_rank = jnp.argsort(sort_order) - starts[flat_ids]
    return src_rows, flat_ids, pair_rank


def expert_ffn(rows_in, w_gate, w_up, w_down):
    gate_proj = jnp.einsum('lscd,ldf->lscf', rows_in, w_gate, preferred_element_type=jnp.float32)
    up_proj = jnp.einsum('lscd,ldf->lscf', rows_in, w_up, preferred_element_type=jnp.float32)
    hidden_act = (jax.nn.silu(gate_proj) * up_proj).astype(jnp.bfloat16)
    return jnp.einsum('lscf,lfd->lscd', hidden_act, w_down, preferred_element_type=jnp.float32).astype(jnp.bfloat16)


def solution(mesh):
    ep_size = mesh.shape['ep']

    def device_body(hidden, route_idx, gate_weights, w_gate, w_up, w_down):
        tok_count, top_k = route_idx.shape
        d_model = hidden.shape[1]
        local_experts = w_gate.shape[0]
        num_experts = local_experts * ep_size
        row_cap = min(tok_count, 4 * top_k * tok_count // num_experts)
        src_rows, flat_ids, pair_rank = pair_plan(route_idx, num_experts, row_cap)
        send_idx = src_rows.reshape(ep_size, local_experts, row_cap).transpose(1, 0, 2)
        send_rows = hidden[send_idx]
        recv_rows = lax.all_to_all(send_rows, 'ep', 1, 1, tiled=True)
        expert_out = expert_ffn(recv_rows, w_gate, w_up, w_down)
        back_rows = lax.all_to_all(expert_out, 'ep', 1, 1, tiled=True)
        slot_pos = (flat_ids % local_experts) * (ep_size * row_cap) + (flat_ids // local_experts) * row_cap + pair_rank
        picked = back_rows.reshape(-1, d_model)[slot_pos].reshape(tok_count, top_k, d_model)
        mixed_out = jnp.sum(gate_weights[:, :, None] * picked, axis=1)
        return mixed_out.astype(jnp.bfloat16)

    row_spec = P(('dp', 'ep'), None)
    expert_spec = P('ep', None, None)
    return jax.shard_map(device_body, mesh=mesh, in_specs=(row_spec, row_spec, row_spec, expert_spec, expert_spec, expert_spec), out_specs=row_spec, check_vma=False)
```

profile of v0, /device:TPU:112, one launch (start us, length us, event | category | flops | bytes accessed | tf_op | source)
XLA Modules:
  0.0 843.0 jit_solution(2593405849931742989)
XLA Ops:
  0.0 0.9 copy.19
  1.2 9.2 %scatter_custom_fusion = s32[64]{0:T(128)S(1)} fusion(s32[1152]{0:T(1024)S(1)} %maximum_reduce_fusion, s32[1152]{0:T(1024)S(1)} %broadcast.236, s32[]{:T(128)} %constant.31.clone.1), kind=kCustom, calls=%fused_computation.109 | custom fusion | flops 1152 | bytes 260 | tf_op jit(solution)/shard_map/scatter-add | solution.py:11
  11.5 5.0 sort.34
  16.5 24.1 %gather_fusion = s32[4608]{0:T(1024)S(1)} fusion(s32[1152]{0:T(1024)S(1)} %get-tuple-element.7, s32[5120]{0:T(1024)S(1)} %pad_clamp_fusion.1), kind=kCustom, calls=%fused_computation | custom fusion | bytes 55296 | tf_op jit(solution)/shard_map/gather | solution.py:15
  41.0 19.7 %gather_fusion.1 = bf16[4608,2560]{1,0:T(8,128)(2,1)} fusion(bf16[192,2560]{1,0:T(8,128)(2,1)S(1)} %copy-done, s32[5120]{0:T(1024)S(1)} %pad_clamp_fusion), kind=kCustom, calls=%fused_computation.1 | custom fusion | bytes 47204352 | tf_op jit(solution)/shard_map/gather | solution.py:38
  60.7 11.5 %copy.23 = bf16[8,8,72,2560]{3,2,0,1:T(8,128)(2,1)S(1)} copy(bf16[8,8,72,2560]{3,2,1,0:T(8,128)(2,1)} %bitcast.100) | data formatting | bytes 47185920 | tf_op jit(solution)/shard_map/gather | solution.py:38
  72.2 262.7 %all_to_all.10 = bf16[8,8,72,2560]{3,2,0,1:T(8,128)(2,1)} all-to-all(bf16[8,8,72,2560]{3,2,0,1:T(8,128)(2,1)S(1)} %copy.23), channel_id=1, replica_groups=mesh['dp'=2,'ep'=8] {'ep'}, dimensions={1} | all-to-all | bytes 47185920 | tf_op jit(solution)/shard_map/all_to_all | solution.py:39
  334.9 52.8 %fusion.2 = f32[8,8,72,1536]{3,2,1,0:T(8,128)} fusion(bf16[8,2560,1536]{2,1,0:T(8,128)(2,1)} %param.10, bf16[8,8,72,2560]{3,2,0,1:T(8,128)(2,1)} %all_to_all.10), kind=kOutput, calls=%fused_computation.6 | convolution fusion | flops 36238786560 | bytes 114819072 | tf_op jit(solution)/shard_map/lscd,ldf->lscf/dot_general | solution.py:22
  387.7 54.6 %multiply_convert_fusion.clone.4 = bf16[8,8,72,1536]{3,2,1,0:T(8,128)(2,1)} fusion(f32[8,8,72,1536]{3,2,1,0:T(8,128)} %fusion.2, bf16[8,2560,1536]{2,1,0:T(8,128)(2,1)} %param.9, bf16[8,8,72,2560]{3,2,0,1:T(8,128)(2,1)} %all_to_all.10), kind=kOutput, calls=%fused_computation.10.clone.clone.clone.1 | convolution fusion | flops 36281253888 | bytes 128974848 | tf_op jit(solution)/shard_map/lscd,ldf->lscf/dot_general | solution.py:21
  442.3 53.1 %fusion.10 = bf16[8,8,72,2560]{3,2,1,0:T(8,128)(2,1)} fusion(bf16[8,1536,2560]{2,1,0:T(8,128)(2,1)} %param.11, bf16[8,8,72,1536]{3,2,1,0:T(8,128)(2,1)} %multiply_convert_fusion.clone.4), kind=kOutput, calls=%fused_computation.13 | convolution fusion | flops 36250583040 | bytes 100663296 | tf_op jit(solution)/shard_map/lscf,lfd->lscd/dot_general | solution.py:24
  495.5 19.6 %copy.26 = bf16[8,8,72,2560]{3,2,0,1:T(8,128)(2,1)} copy(bf16[8,8,72,2560]{3,2,1,0:T(8,128)(2,1)} %fusion.10) | data formatting | bytes 47185920 | tf_op jit(solution)/shard_map/convert_element_type | solution.py:24
  515.1 6.8 all-to-all-start.1
  522.0 5.0 sort.35
  527.9 0.7 fusion.34
  528.6 0.7 fusion.32
  529.3 0.7 fusion.33
  530.1 4.5 fusion.28
  534.5 0.8 compare_reduce_fusion.56
  535.4 35.7 %compare_select_fusion.3 = s32[1152]{0:T(1024)S(1)} fusion(s32[1152]{0:T(1024)S(1)} %get-tuple-element.8, pred[1152]{0:T(1024)(128)(4,1)S(1)} %get-tuple-element.65, pred[1152]{0:T(1024)(128)(4,1)S(1)} %get-tuple-element.64, pred[1152]{0:T(1024)(128)(4,1)S(1)} %get-tuple-element.63, pred[1152]{0:T(1024)(128)(4,1)S(1)} %get-tuple-element.62, ...), kind=kLoop, calls=%fused_computation.21 | loop fusion | flops 96768 | bytes 84324 | tf_op jit(solution)/shard_map/select_n | solution.py:43
  571.1 208.2 %all-to-all-done.1 = bf16[8,8,72,2560]{3,2,0,1:T(8,128)(2,1)} async-done(((bf16[8,8,72,2560]{3,2,0,1:T(8,128)(2,1)}), bf16[8,8,72,2560]{3,2,0,1:T(8,128)(2,1)}, u32[]{:S(2)}, u32[]{:S(2)}) %all-to-all-start.1) | async-done | bytes 23592992 | tf_op jit(solution)/shard_map/all_to_all | solution.py:41
  779.3 19.6 %copy.27 = bf16[8,8,72,2560]{3,2,1,0:T(8,128)(2,1)} copy(bf16[8,8,72,2560]{3,2,0,1:T(8,128)(2,1)} %all-to-all-done.1) | data formatting | bytes 47185920 | tf_op jit(solution)/shard_map/all_to_all | solution.py:41
  798.9 23.5 %gather_fusion.2 = bf16[1152,2560]{1,0:T(8,128)(2,1)} fusion(bf16[4608,2560]{1,0:T(8,128)(2,1)} %bitcast.99, s32[2048]{0:T(1024)S(1)} %pad_clamp_fusion.2), kind=kCustom, calls=%fused_computation.2 | custom fusion | bytes 11801088 | tf_op jit(solution)/shard_map/gather | solution.py:43
  822.4 11.0 %reshape.136 = f32[192,6,2560]{2,1,0:T(8,128)} reshape(bf16[1152,2560]{1,0:T(8,128)(2,1)} %gather_fusion.2) | data formatting | bytes 17694720 | tf_op jit(solution)/shard_map/convert_element_type | solution.py:44
  833.3 9.6 %multiply_reduce_fusion = bf16[192,2560]{1,0:T(8,128)(2,1)} fusion(f32[192,6,2560]{2,1,0:T(8,128)} %reshape.136, f32[192,6]{1,0:T(8,128)S(1)} %copy.18), kind=kLoop, calls=%fused_computation.14 | loop fusion | flops 5406720 | bytes 12784128 | tf_op jit(solution)/shard_map/reduce_sum | solution.py:44
  (46 shorter events, 2.5 us)
Async XLA Ops:
  0.0 41.0 %copy-start = (bf16[192,2560]{1,0:T(8,128)(2,1)S(1)}, bf16[192,2560]{1,0:T(8,128)(2,1)}, u32[]{:S(2)}) copy-start(bf16[192,2560]{1,0:T(8,128)(2,1)} %param.6) | copy-start | bytes 2949124
  1.1 59.6 %copy-start.8 = (s32[1152,1]{0,1:T(1,128)}, s32[1152,1]{0,1:T(1,128)S(1)}, u32[]{:S(2)}) copy-start(s32[1152,1]{0,1:T(1,128)S(1)} %reshape.132) | copy-start | bytes 13828
  1.2 59.5 %copy-start.6 = (s32[1152]{0:T(1024)}, s32[1152]{0:T(1024)S(1)}, u32[]{:S(2)}) copy-start(s32[1152]{0:T(1024)S(1)} %reshape.131) | copy-start | bytes 13828
  10.7 0.5 copy-start.4
  16.5 44.2 %copy-start.2 = (s32[1152]{0:T(1024)}, s32[1152]{0:T(1024)S(1)}, u32[]{:S(2)}) copy-start(s32[1152]{0:T(1024)S(1)} %get-tuple-element.7) | copy-start | bytes 13828
  515.1 6.9 copy-start.3
  515.1 11.9 %copy-start.10 = (f32[192,6]{0,1:T(8,128)S(1)}, f32[192,6]{0,1:T(8,128)}, u32[]{:S(2)}) copy-start(f32[192,6]{0,1:T(8,128)} %param.8) | copy-start | bytes 13828
  515.1 12.1 %copy-start.5 = (s32[64]{0:T(128)S(1)}, s32[64]{0:T(128)}, u32[]{:S(2)}) copy-start(s32[64]{0:T(128)} %copy-done.4) | copy-start | bytes 772
  515.1 14.9 %copy-start.9 = (s32[1152,1]{0,1:T(1,128)S(1)}, s32[1152,1]{0,1:T(1,128)}, u32[]{:S(2)}) copy-start(s32[1152,1]{0,1:T(1,128)} %copy-done.8) | copy-start | bytes 13828
  515.1 20.3 %copy-start.7 = (s32[1152]{0:T(1024)S(1)}, s32[1152]{0:T(1024)}, u32[]{:S(2)}) copy-start(s32[1152]{0:T(1024)} %copy-done.6) | copy-start | bytes 13828
  515.1 264.1 %all-to-all-start.1 = ((bf16[8,8,72,2560]{3,2,0,1:T(8,128)(2,1)}), bf16[8,8,72,2560]{3,2,0,1:T(8,128)(2,1)}, u32[]{:S(2)}, u32[]{:S(2)}) async-start(bf16[8,8,72,2560]{3,2,0,1:T(8,128)(2,1)} %copy.26), calls=%async_computation.1 | async-start | bytes 47185920 | tf_op jit(solution)/shard_map/all_to_all | solution.py:41
  798.9 44.0 %copy-start.1 = (bf16[192,2560]{1,0:T(8,128)(2,1)S(1)}, bf16[192,2560]{1,0:T(8,128)(2,1)}, u32[]{:S(2)}) copy-start(bf16[192,2560]{1,0:T(8,128)(2,1)} %param.6) | copy-start | bytes 2949124
where the time goes:
time: 844 us; the launch traced here: 843 us
  blocking collectives  263 us (31%)
  waiting for transfers between devices  208 us (25%)
  matrix products  161 us (19%)
  local copies, waits for them, and re-layouts  134 us (16%)
  other arithmetic  70.3 us (8%)
    all_to_all x1, blocking collectives, device_body(): recv_rows = lax.all_to_all(send_rows, 'ep', 1, 1, tiled=True)  263 us
    all_to_all x1, waiting for transfers between devices, device_body(): back_rows = lax.all_to_all(expert_out, 'ep', 1, 1, tiled=True)  208 us
    dot_general x1, matrix products, expert_ffn(): jnp.einsum('lscd,ldf->lscf', rows_in, w_gate, preferred_element_type=jnp....  54.6 us
    dot_general x1, matrix products, expert_ffn(): jnp.einsum('lscf,lfd->lscd', hidden_act, w_down, preferred_element_type=j...  53.1 us
    dot_general x1, matrix products, expert_ffn(): jnp.einsum('lscd,ldf->lscf', rows_in, w_up, preferred_element_type=jnp.fl...  52.8 us
    select_n x1, other arithmetic, device_body(): back_rows.reshape(-1, d_model)[slot_pos].reshape(tok_count, top_k, d_model)  35.7 us
    gather x2, local copies, waits for them, and re-layouts, device_body(): send_rows = hidden[send_idx]  31.2 us
    gather x1, local copies, waits for them, and re-layouts, pair_plan(): src_rows = sort_order[pair_pos] // top_k  24.1 us
  transfers between devices with their start and end apart: 1, of which 1 were waited for; matrix products, arithmetic and copies ran while one was open for 6% of the time, Pallas kernels for 0%

commit v1 on v0

v1 whole, which is shorter than its diff:
```python
import functools

import jax
import jax.numpy as jnp
from jax import lax
from jax.experimental import pallas as pl
from jax.experimental.pallas import tpu as pltpu
from jax.sharding import PartitionSpec as P

MESH = pl.DeviceIdType.MESH
BF16 = jnp.bfloat16
F32 = jnp.float32
COL = 256
FCOL = 512
CHUNK = 16
W_SLOTS = 4
D_SLOTS = 8
VMEM_LIMIT = 63_000_000


def ring_places():
    me = lax.axis_index('ep')
    chip = me // 2
    core = lax.rem(me, 2)
    right = lax.rem(chip + 1, 4)
    far = lax.rem(chip + 2, 4)
    left = lax.rem(chip + 3, 4)
    return me, chip, core, right, left, far


def remote(src, dst, send_sem, recv_sem, device):
    return pltpu.make_async_remote_copy(src_ref=src, dst_ref=dst, send_sem=send_sem, recv_sem=recv_sem,
                                        device_id={'ep': device}, device_id_type=MESH)


def dispatch_kernel(tok, cap, win, x_hbm, meta_ref, xs_hbm, c_hbm, cnt_ref,
                    xbuf, mbuf, gbuf, stage, cstage, upper,
                    local_sem, meta_send, meta_recv, plus_send, plus_recv, minus_send, minus_recv,
                    pair_send, pair_recv, xs_sem, c_sem):
    me, chip, core, right, left, far = ring_places()
    n_dev = xbuf.shape[0]
    local_experts, _, pair_rows, d_model = xs_hbm.shape
    tiles = d_model // COL
    half = tiles // 2
    partner = chip * 2 + 1 - core
    right_dev, left_dev = right * 2 + core, left * 2 + core

    own_copy = pltpu.make_async_copy(x_hbm, xbuf.at[me], local_sem.at[0])
    own_copy.start()
    meta_copy = pltpu.make_async_copy(meta_ref, mbuf.at[me], local_sem.at[1])
    meta_copy.start()

    barrier = pltpu.get_barrier_semaphore()
    for k in range(1, n_dev):
        pl.semaphore_signal(barrier, inc=1, device_id={'ep': lax.rem(me + k, n_dev)}, device_id_type=MESH)
    pl.semaphore_wait(barrier, n_dev - 1)

    meta_copy.wait()
    for k in range(1, n_dev):
        remote(mbuf.at[me], mbuf.at[me], meta_send.at[k], meta_recv.at[k], lax.rem(me + k, n_dev)).start()
    own_copy.wait()

    def cols(j):
        return pl.ds(pl.multiple_of(j * COL, COL), COL)

    def block(dev, j):
        return xbuf.at[dev, :, cols(j)]

    def plus(j, slot, dev):
        return remote(block(dev, j), block(dev, j), plus_send.at[slot], plus_recv.at[slot], right_dev)

    def minus(j, slot, dev):
        return remote(block(dev, j), block(dev, j), minus_send.at[slot], minus_recv.at[slot], left_dev)

    def pair(j, group, dev):
        slot = group * tiles + j
        return remote(block(dev, j), block(dev, j), pair_send.at[slot], pair_recv.at[slot], partner)

    def send_own(j, _):
        plus(j, j, me).start()
        other = lax.rem(j + half, tiles)
        minus(other, other, me).start()
        pair(j, 0, me).start()
        return _

    lax.fori_loop(0, tiles, send_own, 0)

    row_i = lax.broadcasted_iota(jnp.int32, upper.shape, 0)
    col_i = lax.broadcasted_iota(jnp.int32, upper.shape, 1)
    same = (row_i < tok) == (col_i < tok)
    upper[...] = jnp.where((row_i < col_i) & same, 1.0, 0.0).astype(BF16)

    for k in range(1, n_dev):
        remote(mbuf.at[me], mbuf.at[lax.rem(me + n_dev - k, n_dev)], meta_send.at[k], meta_recv.at[k], partner).wait_recv()

    def plan(q, counts):
        meta = mbuf[2 * q] + mbuf[2 * q + 1]
        both = meta.shape[1]
        target = (lax.broadcasted_iota(jnp.int32, (local_experts, both), 0) + (me * local_experts + 1)).astype(F32)
        chosen = jnp.zeros((local_experts, both), F32)
        gates = jnp.zeros((local_experts, both), F32)
        for k in range(8):
            hit = jnp.broadcast_to(meta[k:k + 1, :], (local_experts, both)) == target
            chosen = jnp.where(hit, 1.0, chosen)
            gates = jnp.where(hit, jnp.broadcast_to(meta[8 + k:9 + k, :], (local_experts, both)), gates)
        rank = jnp.dot(chosen.astype(BF16), upper[...], preferred_element_type=F32)
        lane = lax.broadcasted_iota(jnp.int32, (local_experts, both), 1)
        first = lane < tok
        place = jnp.where(first, (cap - 1) - rank, cap + rank)
        place = jnp.where(chosen > 0, place, -4096.0)
        count0 = jnp.sum(jnp.where(first, chosen, 0.0), axis=1, keepdims=True)
        count1 = jnp.sum(jnp.where(first, 0.0, chosen), axis=1, keepdims=True)
        out_lane = lax.broadcasted_iota(jnp.int32, counts.shape, 1)
        counts = jnp.where(out_lane == 2 * q, count0, counts)
        counts = jnp.where(out_lane == 2 * q + 1, count1, counts)

        slot_i = lax.broadcasted_iota(jnp.int32, (pair_rows, both), 0).astype(F32)
        for e in range(local_experts):
            gbuf[q, e * pair_rows:(e + 1) * pair_rows, :] = jnp.where(slot_i == place[e:e + 1, :], 1.0, 0.0).astype(BF16)

        turned = jnp.concatenate([place, gates, jnp.zeros((128 - 2 * local_experts, both), F32)], axis=0).T
        for side in range(2):
            part = turned[side * tok:(side + 1) * tok, :]
            offset = 0 if side == 0 else pair_rows - win
            for lt in range(local_experts * win // 128):
                lanes = (lax.broadcasted_iota(jnp.int32, (tok, 128), 1) + lt * 128).astype(F32)
                acc = jnp.zeros((tok, 128), F32)
                for e in range(local_experts):
                    if e * win < (lt + 1) * 128 and (e + 1) * win > lt * 128:
                        acc = jnp.where(lanes == part[:, e:e + 1] + float(e * win - offset),
                                        part[:, local_experts + e:local_experts + e + 1], acc)
                hi = acc.astype(BF16)
                rest = acc - hi.astype(F32)
                mid = rest.astype(BF16)
                low = (rest - mid.astype(F32)).astype(BF16)
                where = slice(lt * 128, (lt + 1) * 128)
                cstage[2 * q + side, 0:tok, where] = hi
                cstage[2 * q + side, tok:2 * tok, where] = mid
                cstage[2 * q + side, 2 * tok:3 * tok, where] = low
        return counts

    counts = lax.fori_loop(0, n_dev // 2, plan, jnp.zeros(cnt_ref.shape, F32))
    cnt_ref[...] = counts.astype(jnp.int32)
    c_copy = pltpu.make_async_copy(cstage, c_hbm, c_sem)
    c_copy.start()

    def xs_copy(q, j):
        return pltpu.make_async_copy(stage.at[q, :, :, cols(j)], xs_hbm.at[:, q, :, cols(j)], xs_sem.at[q, j])

    def pick(q, j):
        rows = xbuf[pl.ds(2 * q, 2), :, cols(j)].reshape(2 * tok, COL)
        hold = local_experts // 2
        for part in range(2):
            sel = gbuf[q, part * hold * pair_rows:(part + 1) * hold * pair_rows, :]
            got = jnp.dot(sel, rows, preferred_element_type=F32).astype(BF16)
            stage[q, part * hold:(part + 1) * hold, :, cols(j)] = got.reshape(hold, pair_rows, COL)
        xs_copy(q, j).start()

    def pick_own(j, _):
        pair(j, 0, partner).wait_recv()
        pick(chip, j)
        return _

    lax.fori_loop(0, tiles, pick_own, 0)

    def near_a(i, _):
        plus(i, i, left_dev).wait_recv()
        plus(i, tiles + i, left_dev).start()
        pair(i, 1, left_dev).start()
        j = half + i
        minus(j, j, right_dev).wait_recv()
        minus(j, tiles + i, right_dev).start()
        pair(j, 2, right_dev).start()
        return _

    lax.fori_loop(0, half, near_a, 0)

    left_other, right_other = left * 2 + 1 - core, right * 2 + 1 - core

    def near_b(i, _):
        j = half + i
        plus(j, j, left_dev).wait_recv()
        pair(j, 1, left_dev).start()
        minus(i, i, right_dev).wait_recv()
        pair(i, 2, right_dev).start()
        pair(i, 1, left_other).wait_recv()
        pick(left, i)
        pair(j, 2, right_other).wait_recv()
        pick(right, j)
        return _

    lax.fori_loop(0, half, near_b, 0)

    far_dev, far_other = far * 2 + core, far * 2 + 1 - core

    def far_c(i, _):
        j = half + i
        plus(i, tiles + i, far_dev).wait_recv()
        pair(i, 3, far_dev).start()
        minus(j, tiles + i, far_dev).wait_recv()
        pair(j, 3, far_dev).start()
        pair(j, 1, left_other).wait_recv()
        pick(left, j)
        pair(i, 2, right_other).wait_recv()
        pick(right, i)
        return _

    lax.fori_loop(0, half, far_c, 0)

    def far_d(i, _):
        j = half + i
        pair(i, 3, far_other).wait_recv()
        pick(far, i)
        pair(j, 3, far_other).wait_recv()
        pick(far, j)
        return _

    lax.fori_loop(0, half, far_d, 0)

    for k in range(1, n_dev):
        remote(mbuf.at[me], mbuf.at[me], meta_send.at[k], meta_recv.at[k], partner).wait_send()

    def drain_ring(s, _):
        plus(0, s, me).wait_send()
        minus(0, s, me).wait_send()
        return _

    lax.fori_loop(0, tiles + half, drain_ring, 0)

    def drain_pair(s, _):
        for group in range(4):
            pair(s, group, me).wait_send()
        for q in range(n_dev // 2):
            xs_copy(q, s).wait()
        return _

    lax.fori_loop(0, tiles, drain_pair, 0)
    c_copy.wait()


def ffn_kernel(cap, cnt_ref, xs_hbm, wg_hbm, wu_hbm, h_hbm, xbuf, gbuf, ubuf, hbuf, zbuf, x_sem, w_sem, h_sem):
    experts, chips, pair_rows, _ = xs_hbm.shape
    d_ff = h_hbm.shape[3]
    f_tiles = d_ff // FCOL
    steps = experts * f_tiles
    per_chip = pair_rows // CHUNK
    all_rows = chips * pair_rows
    zbuf[...] = jnp.zeros_like(zbuf)

    def chunk_range(e, p):
        lo = (cap - cnt_ref[e, 2 * p]) // CHUNK
        hi = (cap + cnt_ref[e, 2 * p + 1] + (CHUNK - 1)) // CHUNK
        return lo, hi

    def chunk(i):
        return pl.ds(pl.multiple_of(i * CHUNK, CHUNK), CHUNK)

    def chunk_total(e):
        total = jnp.int32(0)
        for p in range(chips):
            lo, hi = chunk_range(e, p)
            total = total + (hi - lo)
        return total

    def x_copy(e, p, j, slot, i):
        return pltpu.make_async_copy(xs_hbm.at[e, p, chunk(j), :], xbuf.at[slot, chunk(i), :], x_sem.at[slot, i])

    def start_x(e, slot):
        base = jnp.int32(0)
        for p in range(chips):
            lo, hi = chunk_range(e, p)

            def one(j, _, p=p, lo=lo, base=base):
                x_copy(e, p, j, slot, base + j - lo).start()
                return _

            lax.fori_loop(lo, hi, one, 0)
            base = base + (hi - lo)

    def w_copies(step):
        e, f, slot = step // f_tiles, lax.rem(step, f_tiles), lax.rem(step, W_SLOTS)
        where = pl.ds(pl.multiple_of(f * FCOL, FCOL), FCOL)
        return (pltpu.make_async_copy(wg_hbm.at[e, :, where], gbuf.at[slot], w_sem.at[slot, 0]),
                pltpu.make_async_copy(wu_hbm.at[e, :, where], ubuf.at[slot], w_sem.at[slot, 1]))

    def start_w(step):
        for copy in w_copies(step):
            copy.start()

    def start_h(e, slot):
        base = jnp.int32(0)
        for p in range(chips):
            lo, hi = chunk_range(e, p)

            def one(j, _, p=p, lo=lo, hi=hi, base=base):
                live = (j >= lo) & (j < hi)

                @pl.when(live)
                def _live():
                    pltpu.make_async_copy(hbuf.at[slot, chunk(base + j - lo), :], h_hbm.at[e, p, chunk(j), :],
                                          h_sem.at[slot, p, j]).start()

                @pl.when(jnp.logical_not(live))
                def _dead():
                    pltpu.make_async_copy(zbuf, h_hbm.at[e, p, chunk(j), :], h_sem.at[slot, p, j]).start()

                return _

            lax.fori_loop(0, per_chip, one, 0)
            base = base + (hi - lo)

    def wait_h(slot):
        for p in range(chips):

            def one(j, _, p=p):
                pltpu.make_async_copy(zbuf, h_hbm.at[0, p, chunk(j), :], h_sem.at[slot, p, j]).wait()
                return _

            lax.fori_loop(0, per_chip, one, 0)

    for s in range(min(W_SLOTS, steps)):
        start_w(jnp.int32(s))
        if s == 0:
            start_x(jnp.int32(0), 0)

    sizes = sorted({min(all_rows, m) for m in (128, 192, 256, 384, all_rows)})

    def body(step, _):
        e, f, slot = step // f_tiles, lax.rem(step, f_tiles), lax.rem(step, W_SLOTS)
        side = lax.rem(e, 2)
        total = chunk_total(e)

        @pl.when(f == 0)
        def _enter():
            @pl.when(e + 1 < experts)
            def _next():
                start_x(e + 1, 1 - side)

            def one(i, _):
                x_copy(0, 0, 0, side, i).wait()
                return _

            lax.fori_loop(0, total, one, 0)

            @pl.when(e >= 2)
            def _reuse():
                wait_h(side)

        for copy in w_copies(step):
            copy.wait()
        where = pl.ds(pl.multiple_of(f * FCOL, FCOL), FCOL)
        below = 0
        for size in sizes:
            @pl.when((total > below) & (total <= size // CHUNK))
            def _run(size=size):
                rows = xbuf[side, 0:size, :]
                gate = jnp.dot(rows, gbuf[slot], preferred_element_type=F32)
                up = jnp.dot(rows, ubuf[slot], preferred_element_type=F32)
                hbuf[side, 0:size, where] = (jax.nn.silu(gate) * up).astype(BF16)

            below = size // CHUNK

        @pl.when(step + W_SLOTS < steps)
        def _more():
            start_w(step + W_SLOTS)

        @pl.when(f == f_tiles - 1)
        def _leave():
            start_h(e, side)

        return _

    lax.fori_loop(0, steps, body, 0)
    wait_h(0)
    wait_h(1)


def combine_kernel(tok, win, h_hbm, c_hbm, wd_hbm, out_ref,
                   hbuf, cbuf, wbuf, obuf, ysend, zbuf, pbuf, fbuf, nbuf,
                   h_sem, c_sem, w_sem, y_send, y_recv, far_send, far_recv, near_send, near_recv):
    me, chip, core, right, left, far = ring_places()
    experts, rows, _ = h_hbm.shape
    chips = 4
    pair_rows = rows // chips
    tiles = out_ref.shape[1] // COL
    steps = tiles * experts
    partner = chip * 2 + 1 - core
    right_dev, left_dev = right * 2 + core, left * 2 + core
    dests = (far, right, left, chip)
    cut = tok // 2

    def cols(j):
        return pl.ds(pl.multiple_of(j * COL, COL), COL)

    def w_copy(step):
        t, e, slot = step // experts, lax.rem(step, experts), lax.rem(step, D_SLOTS)
        return pltpu.make_async_copy(wd_hbm.at[e, :, cols(t)], wbuf.at[slot], w_sem.at[slot])

    def h_copy(e):
        return pltpu.make_async_copy(h_hbm.at[e], hbuf.at[e], h_sem.at[e])

    c_copy = pltpu.make_async_copy(c_hbm, cbuf, c_sem)
    for e in range(experts):
        h_copy(e).start()
        if e < D_SLOTS:
            w_copy(jnp.int32(e)).start()
    c_copy.start()

    barrier = pltpu.get_barrier_semaphore()
    for dev in (partner, right_dev, left_dev):
        pl.semaphore_signal(barrier, inc=1, device_id={'ep': dev}, device_id_type=MESH)
    pl.semaphore_wait(barrier, 3)

    def y_copy(t, d):
        return remote(ysend.at[lax.rem(t, 2), d], pbuf.at[t, d], y_send.at[lax.rem(t, 2), d], y_recv.at[t, d], partner)

    def far_copy(t, side):
        src = zbuf.at[lax.rem(t, 3), 0, pl.ds(side * cut, cut), :]
        return remote(src, fbuf.at[t, side], far_send.at[t, side], far_recv.at[t, side], (right_dev, left_dev)[side])

    def near_copy(t, side):
        src = zbuf.at[lax.rem(t, 3), 1 + side]
        return remote(src, nbuf.at[t, side], near_send.at[t, side], near_recv.at[t, side], (right_dev, left_dev)[side])

    def gated(s):
        three = jnp.dot(cbuf[s], obuf[s], preferred_element_type=F32)
        return three[0:tok] + three[tok:2 * tok] + three[2 * tok:3 * tok]

    def project(t):
        def one(e, _):
            step = t * experts + e

            @pl.when(t == 0)
            def _first():
                pltpu.make_async_copy(h_hbm.at[e], hbuf.at[e], h_sem.at[e]).wait()

            w_copy(step).wait()
            o = jnp.dot(hbuf[e], wbuf[lax.rem(step, D_SLOTS)], preferred_element_type=F32).astype(BF16)
            here = pl.ds(pl.multiple_of(e * win, CHUNK), win)
            for p in range(chips):
                obuf[2 * p, here, :] = o[p * pair_rows:p * pair_rows + win]
                obuf[2 * p + 1, here, :] = o[(p + 1) * pair_rows - win:(p + 1) * pair_rows]

            @pl.when(step + D_SLOTS < steps)
            def _more():
                w_copy(step + D_SLOTS).start()

            return _

        lax.fori_loop(0, experts, one, 0)

    def pass_on(t):
        for side in range(2):
            far_copy(t, side).wait_recv()
            part = pl.ds(side * cut, cut)
            zbuf[lax.rem(t, 3), 1 + side, part, :] += fbuf[t, side]
            near_copy(t, side).start()

    def sums(t):
        @pl.when(t >= 2)
        def _reuse():
            for d in range(4):
                y_copy(t - 2, d).wait_send()

        for d in range(4):
            ysend[lax.rem(t, 2), d] = gated(2 * dests[d] + 1 - core)
            y_copy(t, d).start()
        for d in range(4):
            own = gated(2 * dests[d] + core)
            y_copy(t, d).wait_recv()
            zbuf[lax.rem(t, 3), d] = own + pbuf[t, d]
            if d == 0:
                far_copy(t, 0).start()
                far_copy(t, 1).start()

    def finish(t):
        near_copy(t, 0).wait_recv()
        near_copy(t, 1).wait_recv()
        total = zbuf[lax.rem(t, 3), 3] + nbuf[t, 0] + nbuf[t, 1]
        out_ref[:, cols(t)] = total.astype(out_ref.dtype)
        for side in range(2):
            far_copy(t, side).wait_send()
            near_copy(t, side).wait_send()

    def body(t, _):
        @pl.when(t < tiles)
        def _project():
            project(t)

        @pl.when(t == 0)
        def _gates():
            c_copy.wait()

        @pl.when((t >= 1) & (t <= tiles))
        def _pass_on():
            pass_on(t - 1)

        @pl.when(t >= 2)
        def _finish():
            finish(t - 2)

        @pl.when(t < tiles)
        def _sums():
            sums(t)

        return _

    lax.fori_loop(0, tiles + 2, body, 0)
    for back in (2, 1):
        for d in range(4):
            y_copy(jnp.int32(tiles - back), d).wait_send()


def solution(mesh):
    ep_size = mesh.shape['ep']
    chips = ep_size // 2

    def device_body(hidden, route_idx, gate_weights, w_gate, w_up, w_down):
        tok, top_k = route_idx.shape
        d_model = hidden.shape[1]
        experts, _, d_ff = w_gate.shape
        num_experts = experts * ep_size
        cap = min(tok, 4 * top_k * tok // num_experts)
        pair_rows = 2 * cap
        win = (cap + CHUNK - 1) // CHUNK * CHUNK
        tiles = d_model // COL
        rows = chips * pair_rows
        any_space = pl.BlockSpec(memory_space=pl.ANY)
        vmem = pl.BlockSpec(memory_space=pltpu.VMEM)
        dma = pltpu.SemaphoreType.DMA

        core = lax.rem(lax.axis_index('ep'), 2)
        packed = jnp.zeros((2, 8, tok), F32)
        packed = packed.at[0, :top_k].set(route_idx.T.astype(F32) + 1.0).at[1, :top_k].set(gate_weights.T)
        packed = packed.reshape(16, tok)
        blank = jnp.zeros_like(packed)
        meta = jnp.concatenate([jnp.where(core == 0, packed, blank), jnp.where(core == 1, packed, blank)], axis=1)

        xs, gates, counts = pl.pallas_call(
            functools.partial(dispatch_kernel, tok, cap, win),
            out_shape=(jax.ShapeDtypeStruct((experts, chips, pair_rows, d_model), BF16),
                       jax.ShapeDtypeStruct((ep_size, 3 * tok, experts * win), BF16),
                       jax.ShapeDtypeStruct((experts, 128), jnp.int32)),
            in_specs=[any_space, vmem],
            out_specs=(any_space, any_space, vmem),
            scratch_shapes=[
                pltpu.VMEM((ep_size, tok, d_model), BF16),
                pltpu.VMEM((ep_size, 16, 2 * tok), F32),
                pltpu.VMEM((chips, experts * pair_rows, 2 * tok), BF16),
                pltpu.VMEM((chips, experts, pair_rows, d_model), BF16),
                pltpu.VMEM((ep_size, 3 * tok, experts * win), BF16),
                pltpu.VMEM((2 * tok, 2 * tok), BF16),
                dma((2,)), dma((ep_size,)), dma((ep_size,)),
                dma((tiles + tiles // 2,)), dma((tiles + tiles // 2,)), dma((tiles + tiles // 2,)), dma((tiles + tiles // 2,)),
                dma((4 * tiles,)), dma((4 * tiles,)), dma((chips, tiles)), dma,
            ],
            compiler_params=pltpu.CompilerParams(collective_id=0, has_side_effects=True, vmem_limit_bytes=VMEM_LIMIT),
            name='dispatch',
        )(hidden, meta)

        act = pl.pallas_call(
            functools.partial(ffn_kernel, cap),
            out_shape=jax.ShapeDtypeStruct((experts, chips, pair_rows, d_ff), BF16),
            in_specs=[pl.BlockSpec(memory_space=pltpu.SMEM), any_space, any_space, any_space],
            out_specs=any_space,
            scratch_shapes=[
                pltpu.VMEM((2, rows, d_model), BF16),
                pltpu.VMEM((W_SLOTS, d_model, FCOL), BF16),
                pltpu.VMEM((W_SLOTS, d_model, FCOL), BF16),
                pltpu.VMEM((2, rows, d_ff), BF16),
                pltpu.VMEM((CHUNK, d_ff), BF16),
                dma((2, rows // CHUNK)), dma((W_SLOTS, 2)), dma((2, chips, pair_rows // CHUNK)),
            ],
            compiler_params=pltpu.CompilerParams(vmem_limit_bytes=VMEM_LIMIT),
            name='gate_up',
        )(counts, xs, w_gate, w_up)

        return pl.pallas_call(
            functools.partial(combine_kernel, tok, win),
            out_shape=jax.ShapeDtypeStruct((tok, d_model), BF16),
            in_specs=[any_space, any_space, any_space],
            out_specs=vmem,
            scratch_shapes=[
                pltpu.VMEM((experts, rows, d_ff), BF16),
                pltpu.VMEM((ep_size, 3 * tok, experts * win), BF16),
                pltpu.VMEM((D_SLOTS, d_ff, COL), BF16),
                pltpu.VMEM((ep_size, experts * win, COL), BF16),
                pltpu.VMEM((2, chips, tok, COL), F32),
                pltpu.VMEM((3, chips, tok, COL), F32),
                pltpu.VMEM((tiles, chips, tok, COL), F32),
                pltpu.VMEM((tiles, 2, tok // 2, COL), F32),
                pltpu.VMEM((tiles, 2, tok, COL), F32),
                dma((experts,)), dma, dma((D_SLOTS,)),
                dma((2, chips)), dma((tiles, chips)), dma((tiles, 2)), dma((tiles, 2)), dma((tiles, 2)), dma((tiles, 2)),
            ],
            compiler_params=pltpu.CompilerParams(collective_id=1, has_side_effects=True, vmem_limit_bytes=VMEM_LIMIT),
            name='down_combine',
        )(act.reshape(experts, rows, d_ff), gates, w_down)

    row_spec = P(('dp', 'ep'), None)
    expert_spec = P('ep', None, None)
    return jax.shard_map(device_body, mesh=mesh, in_specs=(row_spec, row_spec, row_spec, expert_spec, expert_spec, expert_spec), out_specs=row_spec, check_vma=False)
```

time: 844 us -> 228 us (0.27)
  blocking collectives: 263 us -> 0 us
  Pallas kernels: 0 us -> 224 us
  waiting for transfers between devices: 208 us -> 0 us
  matrix products: 161 us -> 0 us
  local copies, waits for them, and re-layouts: 134 us -> 3.01 us
  other arithmetic: 70.3 us -> 1.39 us
    all_to_all x1 -> x0, blocking collectives: 263 us -> none  [device_body(): recv_rows = lax.all_to_all(send_rows, 'ep', 1, 1, tiled=True)]
    pallas_call x0 -> x3, Pallas kernels: none -> 224 us  [the longest x1 114 us: device_body(): pl.pallas_call(functools.partial(combine_kernel, tok, win), out_shape=jax...]
    all_to_all x1 -> x0, waiting for transfers between devices: 208 us -> none  [device_body(): back_rows = lax.all_to_all(expert_out, 'ep', 1, 1, tiled=True)]
    dot_general x3 -> x0, matrix products: 161 us -> none  [the longest x1 54.6 us: expert_ffn(): jnp.einsum('lscd,ldf->lscf', rows_in, w_gate, preferred_element_type=jnp....]
    gather x8 -> x0, local copies, waits for them, and re-layouts: 81.6 us -> none  [the longest x2 31.2 us: device_body(): send_rows = hidden[send_idx]]
    select_n x3 -> x1, other arithmetic: 35.8 us -> 0.01 us  [device_body(): jnp.where(core == 0, packed, blank)]
    convert_element_type x2 -> x0, local copies, waits for them, and re-layouts: 30.6 us -> none  [the longest x1 19.6 us: expert_ffn(): jnp.einsum('lscf,lfd->lscd', hidden_act, w_down, preferred_element_type=j...]
    all_to_all x1 -> x0, local copies, waits for them, and re-layouts: 19.6 us -> none  [device_body(): back_rows = lax.all_to_all(expert_out, 'ep', 1, 1, tiled=True)]
  transfers between devices with their start and end apart: 1 -> 0, of which waited for: 1 -> 0; matrix products, arithmetic and copies ran while one was open for 6% -> 0% of each run, Pallas kernels for 0% -> 0%
where the time goes in v1:
time: 228 us
  Pallas kernels  224 us (98%)
  local copies, waits for them, and re-layouts  3.01 us (1%)
    pallas_call x1, Pallas kernels, device_body(): pl.pallas_call(functools.partial(combine_kernel, tok, win), out_shape=jax...  114 us
    pallas_call x1, Pallas kernels, device_body(): pl.pallas_call(functools.partial(ffn_kernel, cap), out_shape=jax.ShapeDty...  60.5 us
    pallas_call x1, Pallas kernels, device_body(): pl.pallas_call(functools.partial(dispatch_kernel, tok, cap, win), out_sha...  49.3 us

profile of v1, /device:TPU:112, one launch (start us, length us, event | category | flops | bytes accessed | tf_op | source)
XLA Modules:
  0.0 228.3 jit_solution(8449247667940759529)
XLA Ops:
  0.0 0.7 add_bitcast_fusion
  0.7 0.8 scatter.9
  1.5 0.7 pad_maximum_fusion.meta_ref
  2.2 49.3 %dispatch.1 = (bf16[8,4,144,2560]{3,2,1,0:T(8,128)(2,1)}, bf16[8,576,640]{2,1,0:T(8,128)(2,1)}, s32[8,128]{1,0:T(8,128)}) custom-call(bf16[192,2560]{1,0:T(8,128)(2,1)} %x_hbm.1, f32[16,384]{1,0:T(8,128)} %pad_maximum_fusion.meta_ref), custom_call_target="tpu_custom_call" | custom-call | tf_op jit(solution)/shard_map/dispatch/pallas_call | solution.py:539
  51.5 60.5 %gate_up.1 = bf16[8,4,144,1536]{3,2,1,0:T(8,128)(2,1)} custom-call(s32[8,128]{1,0:T(8,128)} %get-tuple-element.32.cnt_ref, bf16[8,4,144,2560]{3,2,1,0:T(8,128)(2,1)} %get-tuple-element.33.xs_hbm, bf16[8,2560,1536]{2,1,0:T(8,128)(2,1)} %wg_hbm.1, bf16[8,2560,1536]{2,1,0:T(8,128)(2,1)} %wu_hbm.1), custom_call_target="tpu_custom_call" | custom-call | tf_op jit(solution)/shard_map/gate_up/pallas_call | solution.py:561
  112.0 114.0 %down_combine.1 = bf16[192,2560]{1,0:T(8,128)(2,1)} custom-call(bf16[8,576,1536]{2,1,0:T(8,128)(2,1)} %bitcast.12, bf16[8,576,640]{2,1,0:T(8,128)(2,1)} %get-tuple-element.34.c_hbm, bf16[8,1536,2560]{2,1,0:T(8,128)(2,1)} %wd_hbm.1), custom_call_target="tpu_custom_call" | custom-call | tf_op jit(solution)/shard_map/down_combine/pallas_call | solution.py:578
  226.1 2.2 copy.9
  (2 shorter events, 0.0 us)
